TPU v7x, 32 devices: a whole 2x2x4 slice. The times are simulated.
32 devices in a mesh: dp: 8 (over z, y), tensor: 4 (over x, core).
Axes of the slice: x: 2, y: 2, z: 4, core: 2. Of those that a mesh axis runs over, the one named last changes fastest.
Arguments:
- hidden: bfloat16 [128, 4096], P(('dp', 'tensor')), may hold values from -6 to 6
- shortcut: bfloat16 [128, 4096], P('dp'), may hold values from -6 to 6
- expert_ids: int32 [128, 2], P('dp'), may hold values from 0 to 7, all different within a row; in each aligned block of 16 rows (0 to 15, 16 to 31, ...) at most 6 rows name the same one
- route_weight: float32 [128, 2], P('dp'), may hold values from 0.1 to 1
- dense_gain: float32 [4096], replicated, may hold values from 0.5 to 1.5
- moe_gain: float32 [4096], replicated, may hold values from 0.5 to 1.5
- dense_gate: bfloat16 [4096, 8192], P(None, 'dp'), may hold values from -0.09375 to 0.09375
- dense_lift: bfloat16 [4096, 8192], P(None, 'dp'), may hold values from -0.09375 to 0.09375
- dense_down: bfloat16 [8192, 4096], P('dp'), may hold values from -0.0625 to 0.0625
- expert_gate: bfloat16 [4096, 65536], P(None, ('dp', 'tensor')), may hold values from -0.09375 to 0.09375
- expert_lift: bfloat16 [4096, 65536], P(None, ('dp', 'tensor')), may hold values from -0.09375 to 0.09375
- expert_down: bfloat16 [65536, 4096], P(('dp', 'tensor')), may hold values from -0.0625 to 0.0625
Outputs:
- mixed: bfloat16 [128, 4096], P(('dp', 'tensor'))
Inputs may be any that keep to these rules, and one draw needn't show every extreme that they name: `expert_ids`: the 2 experts of a token differ. In each aligned block of 16 rows (the tokens of one index of dp) no expert is named by more than 6 rows, and in every draw some expert is named by exactly 6 rows of some block; every expert is named somewhere.
All inputs are finite; a program needn't handle non-finite values.
Results may differ from a plain program's by a relative error of at most 0.006.
Values may be sent and summed in bfloat16 or wider, within the bound.
A program may use at most 128 MiB of HBM per device.

v0:
```python
import jax
import jax.numpy as jnp
from jax import lax
from jax.sharding import PartitionSpec as P

D = 4096
E = 8
TOP = 2
CAP = 6
EPSILON = 1e-05


def normalize(values_in, gain):
    values = values_in.astype(jnp.float32)
    scale = lax.rsqrt(jnp.mean(values * values, axis=-1, keepdims=True) + EPSILON)
    return (values * scale * gain).astype(jnp.bfloat16)


def local(
    hidden,
    shortcut,
    expert_ids,
    route_weight,
    dense_gain,
    moe_gain,
    dense_gate,
    dense_lift,
    dense_down,
    expert_gate,
    expert_lift,
    expert_down,
):
    normed = normalize(hidden, dense_gain)
    piece = lax.all_gather(normed, "dp", axis=0, tiled=True)
    gate_vals = jnp.dot(piece, dense_gate, preferred_element_type=jnp.float32)
    lift_vals = jnp.dot(piece, dense_lift, preferred_element_type=jnp.float32)
    dense_inner = (jax.nn.silu(gate_vals) * lift_vals).astype(jnp.bfloat16)
    dense_out = lax.psum_scatter(
        jnp.dot(dense_inner, dense_down, preferred_element_type=jnp.float32),
        "dp",
        scatter_dimension=0,
        tiled=True,
    )
    members = lax.axis_size("dp") // E
    token_count = shortcut.shape[0]
    moe_in = normalize(shortcut, moe_gain)
    flat = expert_ids.reshape(token_count * TOP)
    picked = (flat[:, None] == jnp.arange(E, dtype=jnp.int32)[None, :]).astype(jnp.int32)
    before = jnp.cumsum(picked, axis=0) - picked
    places = flat * CAP + jnp.sum(before * picked, axis=1)
    chosen = (places[:, None] == jnp.arange(E * CAP, dtype=jnp.int32)[None, :]).astype(jnp.float32)
    chosen = chosen.reshape(token_count, TOP, E * CAP)
    spread = jnp.sum(chosen, axis=1).astype(jnp.bfloat16)
    weighted = jnp.sum(chosen * route_weight[:, :, None], axis=1)
    buffer = lax.dot_general(
        spread, moe_in, (((0,), (0,)), ((), ())), preferred_element_type=jnp.float32
    )
    buffer = buffer.astype(jnp.bfloat16).reshape(E, CAP, D)
    outgoing = jnp.repeat(buffer, members, axis=0)
    arrived = lax.all_to_all(outgoing, "dp", split_axis=0, concat_axis=0, tiled=True)
    sources, count, width = arrived.shape
    rows_in = arrived.reshape(sources * count, width)
    gate_vals = jnp.dot(rows_in, expert_gate, preferred_element_type=jnp.float32)
    lift_vals = jnp.dot(rows_in, expert_lift, preferred_element_type=jnp.float32)
    inner = (jax.nn.silu(gate_vals) * lift_vals).astype(jnp.bfloat16)
    terms = jnp.dot(inner, expert_down, preferred_element_type=jnp.float32).astype(jnp.bfloat16)
    returned = lax.all_to_all(
        terms.reshape(sources, count, D), "dp", split_axis=0, concat_axis=0, tiled=True
    )
    summed = jnp.sum(returned.astype(jnp.float32).reshape(E, members, CAP, D), axis=1).reshape(
        E * CAP, D
    )
    moe_part = jnp.dot(
        weighted, summed, precision=lax.Precision.HIGHEST, preferred_element_type=jnp.float32
    )
    moe_out = lax.psum_scatter(moe_part, "tensor", scatter_dimension=0, tiled=True)
    return (hidden.astype(jnp.float32) + dense_out + moe_out).astype(jnp.bfloat16)


def solution(mesh):
    in_specs = (
        P(("dp", "tensor"), None),
        P("dp", None),
        P("dp", None),
        P("dp", None),
        P(),
        P(),
        P(None, "dp"),
        P(None, "dp"),
        P("dp", None),
        P(None, ("dp", "tensor")),
        P(None, ("dp", "tensor")),
        P(("dp", "tensor"), None),
    )
    out_specs = P(("dp", "tensor"), None)
    return jax.shard_map(local, mesh=mesh, in_specs=in_specs, out_specs=out_specs, check_vma=False)
```

profile of v0, /device:TPU:0, one launch (start us, length us, event | category | flops | bytes accessed | tf_op | source)
XLA Modules:
  0.0 215.8 jit_solution(18423160063778586891)
XLA Ops:
  6.5 0.8 copy.29
  7.3 0.1 eq.29
  7.4 0.1 fusion.27
  7.5 0.1 reduce_window_sum.11
  7.5 0.2 select_reduce_fusion.1
  7.7 0.1 reduce_sum.53
  7.8 0.1 copy.30
  7.9 0.7 multiply_add_fusion
  8.6 1.0 fusion.8
  9.6 0.8 convert_reduce_fusion
  10.4 1.2 convolution_convert_fusion.1
  11.6 0.9 reshape_broadcast_in_dim_reshape.3
  12.5 7.3 %all-to-all-start = ((bf16[8,6,4096]{2,1,0:T(8,128)(2,1)}), bf16[8,6,4096]{2,1,0:T(8,128)(2,1)S(1)}, u32[]{:S(2)}, u32[]{:S(2)}) async-start(bf16[8,6,4096]{2,1,0:T(8,128)(2,1)} %reshape_broadcast_in_dim_reshape.3), calls=%async_computation | async-start | bytes 1048576 | tf_op jit(solution)/shard_map/all_to_all | solution.py:60
  19.8 0.9 fusion.20
  20.8 0.9 fusion.26
  21.6 36.0 %all-gather = bf16[8,4,4096]{2,1,0:T(4,128)(2,1)S(1)} all-gather(bf16[1,4,4096]{2,1,0:T(4,128)(2,1)S(1)} %fusion.26), channel_id=1, replica_groups=mesh['dp'=8,'tensor'=4] {'dp'}, dimensions={0}, use_global_device_ids=true | all-gather | bytes 294912 | tf_op jit(solution)/shard_map/all_gather | solution.py:34
  57.6 0.1 reshape.55
  57.7 4.9 %fusion.31 = f32[32,1024]{1,0:T(8,128)S(1)} fusion(bf16[32,4096]{1,0:T(8,128)(2,1)S(1)} %reshape.55, bf16[4096,1024]{1,0:T(8,128)(2,1)} %param.18), kind=kOutput, calls=%fused_computation.47 | convolution fusion | flops 268435456 | bytes 8781824 | tf_op jit(solution)/shard_map/dot_general | solution.py:35
  62.6 0.1 reshape.51
  62.8 8.8 %fusion.32 = f32[48,2048]{1,0:T(8,128)S(1)} fusion(bf16[48,4096]{1,0:T(8,128)(2,1)S(1)} %reshape.51, bf16[4096,2048]{1,0:T(8,128)(2,1)} %param.21), kind=kOutput, calls=%fused_computation.48 | convolution fusion | flops 805306368 | bytes 17563648 | tf_op jit(solution)/shard_map/dot_general | solution.py:63
  71.5 13.7 %convolution_convert_fusion = bf16[48,4096]{1,0:T(8,128)(2,1)S(1)} fusion(bf16[2048,4096]{1,0:T(8,128)(2,1)} %param.23, bf16[48,4096]{1,0:T(8,128)(2,1)S(1)} %reshape.51, bf16[4096,2048]{1,0:T(8,128)(2,1)} %param.22, f32[48,2048]{1,0:T(8,128)S(1)} %fusion.32), kind=kOutput, calls=%fused_computation | convolution fusion | flops 1611399168 | bytes 34734080 | tf_op jit(solution)/shard_map/dot_general | solution.py:66
  85.3 1.0 reshape.52
  86.2 3.5 %all-to-all-start.1 = ((bf16[8,6,4096]{2,1,0:T(8,128)(2,1)}), bf16[8,6,4096]{2,1,0:T(8,128)(2,1)S(1)}, u32[]{:S(2)}, u32[]{:S(2)}) async-start(bf16[8,6,4096]{2,1,0:T(8,128)(2,1)} %reshape.52), calls=%async_computation.1 | async-start | bytes 1048576 | tf_op jit(solution)/shard_map/all_to_all | solution.py:67
  89.8 9.6 %fusion.2 = f32[32,4096]{1,0:T(8,128)} fusion(bf16[1024,4096]{1,0:T(8,128)(2,1)} %param.20, bf16[32,4096]{1,0:T(8,128)(2,1)S(1)} %reshape.55, bf16[4096,1024]{1,0:T(8,128)(2,1)} %param.19, f32[32,1024]{1,0:T(8,128)S(1)} %fusion.31), kind=kOutput, calls=%fused_computation.6 | convolution fusion | flops 537067520 | bytes 17694720 | tf_op jit(solution)/shard_map/dot_general | solution.py:39
  99.4 0.5 all-to-all-done.1
  99.9 0.1 reshape.53
  100.1 1.0 fusion.33
  101.1 0.6 dynamic-slice
  101.7 0.6 dynamic-slice.2
  103.6 70.0 %all-reduce.5.cloned.1.call-done = f32[32,4096]{1,0:T(8,128)} async-done(((f32[32,4096]{1,0:T(8,128)}), f32[32,4096]{1,0:T(8,128)}) %all-reduce.5.cloned.1.call-update) | async-done | bytes 524304
  173.6 33.8 %all-reduce.7.cloned.1.call-done = f32[16,4096]{1,0:T(8,128)} async-done(((f32[16,4096]{1,0:T(8,128)}), f32[16,4096]{1,0:T(8,128)}) %all-reduce.7.cloned.1.call-update) | async-done | bytes 262160
  207.4 1.6 fusion.24
  (13 shorter events, 0.2 us)
Async XLA Ops:
  12.5 50.1 %all-to-all-start = ((bf16[8,6,4096]{2,1,0:T(8,128)(2,1)}), bf16[8,6,4096]{2,1,0:T(8,128)(2,1)S(1)}, u32[]{:S(2)}, u32[]{:S(2)}) async-start(bf16[8,6,4096]{2,1,0:T(8,128)(2,1)} %reshape_broadcast_in_dim_reshape.3), calls=%async_computation | async-start | bytes 1048576 | tf_op jit(solution)/shard_map/all_to_all | solution.py:60
  85.2 15.9 %copy-start.2 = (u32[32]{0:T(128)S(1)}, u32[32]{0:T(128)}, u32[]{:S(2)}) copy-start(u32[32]{0:T(128)} %constant.27) | copy-start | bytes 388
  85.2 16.5 %copy-start.1 = (u32[32]{0:T(128)S(1)}, u32[32]{0:T(128)}, u32[]{:S(2)}) copy-start(u32[32]{0:T(128)} %constant.31) | copy-start | bytes 388
  85.2 122.1 %copy-start = (bf16[4,4096]{1,0:T(4,128)(2,1)S(1)}, bf16[4,4096]{1,0:T(4,128)(2,1)}, u32[]{:S(2)}) copy-start(bf16[4,4096]{1,0:T(4,128)(2,1)} %param.12) | copy-start | bytes 98308
  86.2 13.7 %all-to-all-start.1 = ((bf16[8,6,4096]{2,1,0:T(8,128)(2,1)}), bf16[8,6,4096]{2,1,0:T(8,128)(2,1)S(1)}, u32[]{:S(2)}, u32[]{:S(2)}) async-start(bf16[8,6,4096]{2,1,0:T(8,128)(2,1)} %reshape.52), calls=%async_computation.1 | async-start | bytes 1048576 | tf_op jit(solution)/shard_map/all_to_all | solution.py:67
  89.7 83.8 %all-reduce.5.cloned.1.call-start = ((), (), s32[]{:S(2)}) async-start(), calls=%async_computation.2 | async-start | bytes 1048576
  99.4 108.0 %all-reduce.7.cloned.1.call-start = ((), (), s32[]{:S(2)}) async-start(), calls=%async_computation.3 | async-start | bytes 524288
Sparse Core Ops, SparseCore 0:
  99.5 73.9 all-reduce.4
  175.9 31.4 all-reduce.6
where the time goes:
time: 216 us
  waiting for transfers between devices  104 us (48%)
  matrix products  39.2 us (18%)
  blocking collectives  36 us (17%)
  between operations  14.8 us (7%)
  starting transfers between devices  10.9 us (5%)
  other arithmetic  6.21 us (3%)
  local copies, waits for them, and re-layouts  4.44 us (2%)
    unnamed x4, waiting for transfers between devices  104 us
    all_gather x1, blocking collectives, local(): piece = lax.all_gather(normed, 'dp', axis=0, tiled=True)  36 us
    dot_general x1, matrix products, local(): jnp.dot(inner, expert_down, preferred_element_type=jnp.float32)  13.7 us
    dot_general x1, matrix products, local(): jnp.dot(dense_inner, dense_down, preferred_element_type=jnp.float32)  9.6 us
    dot_general x1, matrix products, local(): jnp.dot(rows_in, expert_gate, preferred_element_type=jnp.float32)  8.79 us
    all_to_all x1, starting transfers between devices, local(): lax.all_to_all(outgoing, 'dp', split_axis=0, concat_axis=0, tiled=True)  7.31 us
    dot_general x1, matrix products, local(): gate_vals = jnp.dot(piece, dense_gate, preferred_element_type=jnp.float32)  4.92 us
  transfers between devices with their start and end apart: 4, of which 3 were waited for; matrix products, arithmetic and copies ran while one was open for 9% of the time, Pallas kernels for 0%

commit v1 on v0

--- a/solution.py
+++ b/solution.py
@@ -31,7 +31,12 @@
     expert_down,
 ):
     normed = normalize(hidden, dense_gain)
-    piece = lax.all_gather(normed, "dp", axis=0, tiled=True)
+    ring = [normed]
+    for hop in range(7):
+        ring.append(lax.ppermute(ring[-1], "dp", [(dev, (dev + 1) % 8) for dev in range(8)]))
+    piece = jnp.roll(
+        jnp.concatenate(ring[::-1], axis=0), (lax.axis_index("dp") + 1) * ring[0].shape[0], axis=0
+    )
     gate_vals = jnp.dot(piece, dense_gate, preferred_element_type=jnp.float32)
     lift_vals = jnp.dot(piece, dense_lift, preferred_element_type=jnp.float32)
     dense_inner = (jax.nn.silu(gate_vals) * lift_vals).astype(jnp.bfloat16)

time: 216 us -> 222 us (1.028)
  waiting for transfers between devices: 104 us -> 142 us
  blocking collectives: 36 us -> 0 us
  starting transfers between devices: 10.9 us -> 14.7 us
    ppermute x0 -> x7, waiting for transfers between devices: none -> 37.5 us  [local(): lax.ppermute(ring[-1], 'dp', [(dev, (dev + 1) % 8) for dev in range(8)])]
    all_gather x1 -> x0, blocking collectives: 36 us -> none  [local(): piece = lax.all_gather(normed, 'dp', axis=0, tiled=True)]
    ppermute x0 -> x7, starting transfers between devices: none -> 5.08 us  [local(): lax.ppermute(ring[-1], 'dp', [(dev, (dev + 1) % 8) for dev in range(8)])]
  transfers between devices with their start and end apart: 4 -> 11, of which waited for: 3 -> 9; matrix products, arithmetic and copies ran while one was open for 9% -> 10% of each run, Pallas kernels for 0% -> 0%
where the time goes in v1:
time: 222 us; the launch traced here: 221 us
  waiting for transfers between devices  142 us (64%)
  matrix products  39.2 us (18%)
  between operations  14.8 us (7%)
  starting transfers between devices  14.7 us (7%)
  other arithmetic  6.2 us (3%)
  local copies, waits for them, and re-layouts  4.76 us (2%)
    unnamed x4, waiting for transfers between devices  104 us
    ppermute x7, waiting for transfers between devices, local(): lax.ppermute(ring[-1], 'dp', [(dev, (dev + 1) % 8) for dev in range(8)])  37.5 us
    dot_general x1, matrix products, local(): jnp.dot(inner, expert_down, preferred_element_type=jnp.float32)  13.7 us
    dot_general x1, matrix products, local(): jnp.dot(dense_inner, dense_down, preferred_element_type=jnp.float32)  9.6 us
    dot_general x1, matrix products, local(): jnp.dot(rows_in, expert_gate, preferred_element_type=jnp.float32)  8.79 us
    all_to_all x1, starting transfers between devices, local(): lax.all_to_all(outgoing, 'dp', split_axis=0, concat_axis=0, tiled=True)  6 us
    ppermute x7, starting transfers between devices, local(): lax.ppermute(ring[-1], 'dp', [(dev, (dev + 1) % 8) for dev in range(8)])  5.08 us
    dot_general x1, matrix products, local(): lift_vals = jnp.dot(piece, dense_lift, preferred_element_type=jnp.float32)  4.92 us
  transfers between devices with their start and end apart: 11, of which 9 were waited for; matrix products, arithmetic and copies ran while one was open for 10% of the time, Pallas kernels for 0%

profile of v1, /device:TPU:0, one launch (start us, length us, event | category | flops | bytes accessed | tf_op | source)
XLA Modules:
  0.0 221.4 jit_solution(14129256722780771900)
XLA Ops:
  6.5 0.9 fusion.17
  7.4 0.9 fusion.19
  8.3 3.0 %collective-permute-start = (bf16[4,4096]{1,0:T(4,128)(2,1)S(1)}, bf16[4,4096]{1,0:T(4,128)(2,1)S(1)}, u32[]{:S(2)}, u32[]{:S(2)}) collective-permute-start(bf16[4,4096]{1,0:T(4,128)(2,1)S(1)} %fusion.19), channel_id=1, source_target_pairs={{0,4},{4,8},{8,12},{12,16},{16,20},{20,24},{24,28},{28,0},{1,5},{5... | collective-permute-start | bytes 98312 | tf_op jit(solution)/shard_map/ppermute | solution.py:36
  11.4 0.8 copy.29
  12.3 0.2 select_reduce_fusion.1
  12.7 0.7 multiply_add_fusion
  13.4 1.0 fusion.6
  14.4 1.8 collective-permute-done
  16.3 0.8 convert_reduce_fusion
  17.0 5.8 %collective-permute-done.1 = bf16[4,4096]{1,0:T(4,128)(2,1)S(1)} collective-permute-done((bf16[4,4096]{1,0:T(4,128)(2,1)S(1)}, bf16[4,4096]{1,0:T(4,128)(2,1)S(1)}, u32[]{:S(2)}, u32[]{:S(2)}) %collective-permute-start.1) | collective-permute-done | bytes 32800 | tf_op jit(solution)/shard_map/ppermute | solution.py:36
  22.9 1.2 convolution_convert_fusion.1
  24.1 0.9 reshape_broadcast_in_dim_reshape.3
  25.0 6.0 %all-to-all-start = ((bf16[8,6,4096]{2,1,0:T(8,128)(2,1)}), bf16[8,6,4096]{2,1,0:T(8,128)(2,1)S(1)}, u32[]{:S(2)}, u32[]{:S(2)}) async-start(bf16[8,6,4096]{2,1,0:T(8,128)(2,1)} %reshape_broadcast_in_dim_reshape.3), calls=%async_computation | async-start | bytes 1048576 | tf_op jit(solution)/shard_map/all_to_all | solution.py:65
  31.0 2.0 collective-permute-start.3
  33.1 10.0 %collective-permute-done.3 = bf16[4,4096]{1,0:T(4,128)(2,1)S(1)} collective-permute-done((bf16[4,4096]{1,0:T(4,128)(2,1)S(1)}, bf16[4,4096]{1,0:T(4,128)(2,1)S(1)}, u32[]{:S(2)}, u32[]{:S(2)}) %collective-permute-start.3) | collective-permute-done | bytes 32800 | tf_op jit(solution)/shard_map/ppermute | solution.py:36
  43.1 6.6 %collective-permute-done.4 = bf16[4,4096]{1,0:T(4,128)(2,1)S(1)} collective-permute-done((bf16[4,4096]{1,0:T(4,128)(2,1)S(1)}, bf16[4,4096]{1,0:T(4,128)(2,1)S(1)}, u32[]{:S(2)}, u32[]{:S(2)}) %collective-permute-start.4) | collective-permute-done | bytes 32800 | tf_op jit(solution)/shard_map/ppermute | solution.py:36
  49.7 6.6 %collective-permute-done.5 = bf16[4,4096]{1,0:T(4,128)(2,1)S(1)} collective-permute-done((bf16[4,4096]{1,0:T(4,128)(2,1)S(1)}, bf16[4,4096]{1,0:T(4,128)(2,1)S(1)}, u32[]{:S(2)}, u32[]{:S(2)}) %collective-permute-start.5) | collective-permute-done | bytes 32800 | tf_op jit(solution)/shard_map/ppermute | solution.py:36
  56.3 6.6 %collective-permute-done.6 = bf16[4,4096]{1,0:T(4,128)(2,1)S(1)} collective-permute-done((bf16[4,4096]{1,0:T(4,128)(2,1)S(1)}, bf16[4,4096]{1,0:T(4,128)(2,1)S(1)}, u32[]{:S(2)}, u32[]{:S(2)}) %collective-permute-start.6) | collective-permute-done | bytes 32800 | tf_op jit(solution)/shard_map/ppermute | solution.py:36
  62.9 0.4 concatenate.6
  63.3 4.9 %fusion.9 = f32[32,1024]{1,0:T(8,128)S(1)} fusion(bf16[4096,1024]{1,0:T(8,128)(2,1)} %param.19, bf16[64,4096]{1,0:T(8,128)(2,1)S(1)} %concatenate.6, s32[]{:T(128)S(6)} %select_n.14), kind=kOutput, calls=%fused_computation.14 | convolution fusion | flops 268435456 | bytes 8781828 | tf_op jit(solution)/shard_map/dot_general | solution.py:41
  68.4 8.8 %fusion.35 = f32[48,2048]{1,0:T(8,128)S(1)} fusion(bf16[48,4096]{1,0:T(8,128)(2,1)S(1)} %reshape.51, bf16[4096,2048]{1,0:T(8,128)(2,1)} %param.21), kind=kOutput, calls=%fused_computation.46 | convolution fusion | flops 805306368 | bytes 17563648 | tf_op jit(solution)/shard_map/dot_general | solution.py:68
  77.2 13.7 %convolution_convert_fusion = bf16[48,4096]{1,0:T(8,128)(2,1)S(1)} fusion(bf16[2048,4096]{1,0:T(8,128)(2,1)} %param.23, bf16[48,4096]{1,0:T(8,128)(2,1)S(1)} %reshape.51, bf16[4096,2048]{1,0:T(8,128)(2,1)} %param.22, f32[48,2048]{1,0:T(8,128)S(1)} %fusion.35), kind=kOutput, calls=%fused_computation | convolution fusion | flops 1611399168 | bytes 34734080 | tf_op jit(solution)/shard_map/dot_general | solution.py:71
  90.9 1.0 reshape.52
  91.8 3.5 %all-to-all-start.1 = ((bf16[8,6,4096]{2,1,0:T(8,128)(2,1)}), bf16[8,6,4096]{2,1,0:T(8,128)(2,1)S(1)}, u32[]{:S(2)}, u32[]{:S(2)}) async-start(bf16[8,6,4096]{2,1,0:T(8,128)(2,1)} %reshape.52), calls=%async_computation.1 | async-start | bytes 1048576 | tf_op jit(solution)/shard_map/all_to_all | solution.py:72
  95.4 9.6 %fusion.22 = f32[32,4096]{1,0:T(8,128)} fusion(bf16[1024,4096]{1,0:T(8,128)(2,1)} %param.20, f32[32,1024]{1,0:T(8,128)S(1)} %fusion.9, bf16[4096,1024]{1,0:T(8,128)(2,1)} %param.18, bf16[64,4096]{1,0:T(8,128)(2,1)S(1)} %concatenate.6, s32[]{:T(128)S(6)} %select_n.14), kind=kOutput, calls=%fused_computation.30 | convolution fusion | flops 537067520 | bytes 17694724 | tf_op jit(solution)/shard_map/dot_general | solution.py:44
  105.1 0.5 all-to-all-done.1
  105.7 1.0 fusion.36
  106.7 0.6 dynamic-slice.2
  107.3 0.6 dynamic-slice
  109.2 70.0 %all-reduce.5.cloned.1.call-done = f32[32,4096]{1,0:T(8,128)} async-done(((f32[32,4096]{1,0:T(8,128)}), f32[32,4096]{1,0:T(8,128)}) %all-reduce.5.cloned.1.call-update) | async-done | bytes 524304
  179.2 33.8 %all-reduce.7.cloned.1.call-done = f32[16,4096]{1,0:T(8,128)} async-done(((f32[16,4096]{1,0:T(8,128)}), f32[16,4096]{1,0:T(8,128)}) %all-reduce.7.cloned.1.call-update) | async-done | bytes 262160
  213.0 1.6 fusion.21
  (26 shorter events, 0.8 us)
Async XLA Ops:
  8.3 8.0 %collective-permute-start = (bf16[4,4096]{1,0:T(4,128)(2,1)S(1)}, bf16[4,4096]{1,0:T(4,128)(2,1)S(1)}, u32[]{:S(2)}, u32[]{:S(2)}) collective-permute-start(bf16[4,4096]{1,0:T(4,128)(2,1)S(1)} %fusion.19), channel_id=1, source_target_pairs={{0,4},{4,8},{8,12},{12,16},{16,20},{20,24},{24,28},{28,0},{1,5},{5... | collective-permute-start | bytes 98312 | tf_op jit(solution)/shard_map/ppermute | solution.py:36
  16.3 6.6 %collective-permute-start.1 = (bf16[4,4096]{1,0:T(4,128)(2,1)S(1)}, bf16[4,4096]{1,0:T(4,128)(2,1)S(1)}, u32[]{:S(2)}, u32[]{:S(2)}) collective-permute-start(bf16[4,4096]{1,0:T(4,128)(2,1)S(1)} %collective-permute-done), channel_id=1, source_target_pairs={{0,4},{4,8},{8,12},{12,16},{16,20},{20,24},{24,28},{28,0},{1,5},{5... | collective-permute-start | bytes 98312 | tf_op jit(solution)/shard_map/ppermute | solution.py:36
  22.9 8.1 %collective-permute-start.2 = (bf16[4,4096]{1,0:T(4,128)(2,1)S(1)}, bf16[4,4096]{1,0:T(4,128)(2,1)S(1)}, u32[]{:S(2)}, u32[]{:S(2)}) collective-permute-start(bf16[4,4096]{1,0:T(4,128)(2,1)S(1)} %collective-permute-done.1), channel_id=1, source_target_pairs={{0,4},{4,8},{8,12},{12,16},{16,20},{20,24},{24,28},{28,0},{1,5},{5... | collective-permute-start | bytes 98312 | tf_op jit(solution)/shard_map/ppermute | solution.py:36
  25.0 43.2 %all-to-all-start = ((bf16[8,6,4096]{2,1,0:T(8,128)(2,1)}), bf16[8,6,4096]{2,1,0:T(8,128)(2,1)S(1)}, u32[]{:S(2)}, u32[]{:S(2)}) async-start(bf16[8,6,4096]{2,1,0:T(8,128)(2,1)} %reshape_broadcast_in_dim_reshape.3), calls=%async_computation | async-start | bytes 1048576 | tf_op jit(solution)/shard_map/all_to_all | solution.py:65
  31.0 12.0 %collective-permute-start.3 = (bf16[4,4096]{1,0:T(4,128)(2,1)S(1)}, bf16[4,4096]{1,0:T(4,128)(2,1)S(1)}, u32[]{:S(2)}, u32[]{:S(2)}) collective-permute-start(bf16[4,4096]{1,0:T(4,128)(2,1)S(1)} %collective-permute-done.2), channel_id=1, source_target_pairs={{0,4},{4,8},{8,12},{12,16},{16,20},{20,24},{24,28},{28,0},{1,5},{5... | collective-permute-start | bytes 98312 | tf_op jit(solution)/shard_map/ppermute | solution.py:36
  43.1 6.6 %collective-permute-start.4 = (bf16[4,4096]{1,0:T(4,128)(2,1)S(1)}, bf16[4,4096]{1,0:T(4,128)(2,1)S(1)}, u32[]{:S(2)}, u32[]{:S(2)}) collective-permute-start(bf16[4,4096]{1,0:T(4,128)(2,1)S(1)} %collective-permute-done.3), channel_id=1, source_target_pairs={{0,4},{4,8},{8,12},{12,16},{16,20},{20,24},{24,28},{28,0},{1,5},{5... | collective-permute-start | bytes 98312 | tf_op jit(solution)/shard_map/ppermute | solution.py:36
  49.7 6.6 %collective-permute-start.5 = (bf16[4,4096]{1,0:T(4,128)(2,1)S(1)}, bf16[4,4096]{1,0:T(4,128)(2,1)S(1)}, u32[]{:S(2)}, u32[]{:S(2)}) collective-permute-start(bf16[4,4096]{1,0:T(4,128)(2,1)S(1)} %collective-permute-done.4), channel_id=1, source_target_pairs={{0,4},{4,8},{8,12},{12,16},{16,20},{20,24},{24,28},{28,0},{1,5},{5... | collective-permute-start | bytes 98312 | tf_op jit(solution)/shard_map/ppermute | solution.py:36
  56.3 6.6 %collective-permute-start.6 = (bf16[4,4096]{1,0:T(4,128)(2,1)S(1)}, bf16[4,4096]{1,0:T(4,128)(2,1)S(1)}, u32[]{:S(2)}, u32[]{:S(2)}) collective-permute-start(bf16[4,4096]{1,0:T(4,128)(2,1)S(1)} %collective-permute-done.5), channel_id=1, source_target_pairs={{0,4},{4,8},{8,12},{12,16},{16,20},{20,24},{24,28},{28,0},{1,5},{5... | collective-permute-start | bytes 98312 | tf_op jit(solution)/shard_map/ppermute | solution.py:36
  90.8 15.9 %copy-start.2 = (u32[32]{0:T(128)S(1)}, u32[32]{0:T(128)}, u32[]{:S(2)}) copy-start(u32[32]{0:T(128)} %constant.62) | copy-start | bytes 388
  90.9 16.4 %copy-start.1 = (u32[32]{0:T(128)S(1)}, u32[32]{0:T(128)}, u32[]{:S(2)}) copy-start(u32[32]{0:T(128)} %constant.58) | copy-start | bytes 388
  90.9 122.1 %copy-start = (bf16[4,4096]{1,0:T(4,128)(2,1)S(1)}, bf16[4,4096]{1,0:T(4,128)(2,1)}, u32[]{:S(2)}) copy-start(bf16[4,4096]{1,0:T(4,128)(2,1)} %param.12) | copy-start | bytes 98308
  91.8 13.7 %all-to-all-start.1 = ((bf16[8,6,4096]{2,1,0:T(8,128)(2,1)}), bf16[8,6,4096]{2,1,0:T(8,128)(2,1)S(1)}, u32[]{:S(2)}, u32[]{:S(2)}) async-start(bf16[8,6,4096]{2,1,0:T(8,128)(2,1)} %reshape.52), calls=%async_computation.1 | async-start | bytes 1048576 | tf_op jit(solution)/shard_map/all_to_all | solution.py:72
  95.3 83.8 %all-reduce.5.cloned.1.call-start = ((), (), s32[]{:S(2)}) async-start(), calls=%async_computation.2 | async-start | bytes 1048576
  105.0 108.0 %all-reduce.7.cloned.1.call-start = ((), (), s32[]{:S(2)}) async-start(), calls=%async_computation.3 | async-start | bytes 524288
Sparse Core Ops, SparseCore 0:
  105.1 73.9 all-reduce.4
  181.5 31.4 all-reduce.6
